TPU v7x, 256 devices: a whole 4x4x8 slice. The times are simulated.
256 devices in a mesh: gx: 16 (over x, z_lo, core), gy: 4 (over y), gz: 4 (over z_hi).
Axes of the slice: x: 4, y: 4, z: 8 (z_hi: 4, z_lo: 2; z = z_hi * 2 + z_lo), core: 2. Of those that a mesh axis runs over, the one named last changes fastest.
Arguments:
- right_side: float32 [4, 5, 16, 32, 512], P(None, None, 'gx', 'gy', 'gz'), may hold values from -6 to 6
- jacobian: bfloat16 [27, 5, 5, 16, 32, 512], P(None, None, None, 'gx', 'gy', 'gz'), may hold values from -0.14 to 12.14, as said below
Outputs:
- solution: float32 [4, 5, 16, 32, 512], P(None, None, 'gx', 'gy', 'gz')
- residual: float32 [4, 5, 16, 32, 512], P(None, None, 'gx', 'gy', 'gz')
Inputs may be any that keep to these rules, and one draw needn't show every extreme that they name: `jacobian`: blocks of offsets other than 13 and the off-diagonal entries of block 13 lie within -0.14 to 0.14; the diagonal entries of block 13 exceed 5.8 in every cell.
All inputs are finite; a program needn't handle non-finite values.
Results may differ from a plain program's by a relative error of at most 0.0003.
Values sent between devices are 32-bit elements.
A program may use at most 64 MiB of HBM per device.

v0:
```python
import functools

import jax
import jax.numpy as jnp
from jax import lax
from jax.sharding import Mesh
from jax.sharding import PartitionSpec as P

ITERS = 3
GX_GY_GZ = ("gx_0", "gx_1", "gx_2", "gy", "gz")
GX = ("gx_0", "gx_1", "gx_2")


def extended(cells, sides, width):
    for axis, dim in sides:
        count = lax.axis_size(axis)
        head = lax.slice_in_dim(cells, 0, width, axis=dim)
        tail = lax.slice_in_dim(cells, cells.shape[dim] - width, cells.shape[dim], axis=dim)
        cells = jnp.concatenate(
            [
                lax.ppermute(tail, axis, [(i, (i + 1) % count) for i in range(count)]),
                cells,
                lax.ppermute(head, axis, [((i + 1) % count, i) for i in range(count)]),
            ],
            axis=dim,
        )
    return cells


def one_axis_at_a_time(value, axes):
    return functools.reduce(lax.psum, axes, value)


def dot_high(left, right):
    return jnp.dot(left, right, precision=lax.Precision.HIGHEST, preferred_element_type=jnp.float32)


def lower_solve(factor, target):
    solved = []
    for row_pos in range(factor.shape[0]):
        accum = target[row_pos]
        for prior in range(row_pos):
            accum = accum - factor[row_pos, prior] * solved[prior]
        solved.append(accum / factor[row_pos, row_pos])
    return jnp.stack(solved)


def upper_solve(factor, target):
    size_all = factor.shape[0]
    solved = [None] * size_all
    for row_pos in range(size_all - 1, -1, -1):
        accum = target[row_pos]
        for later in range(row_pos + 1, size_all):
            accum = accum - factor[later, row_pos] * solved[later]
        solved[row_pos] = accum / factor[row_pos, row_pos]
    return jnp.stack(solved)


def extend(field):
    padded = extended(field, ((GX, 2), ("gy", 3), ("gz", 4)), 1)
    position = lax.axis_index("gz")
    bottom = jnp.where(position == 0, 0.0, 1.0).astype(jnp.float32)
    topmost = jnp.where(position == lax.axis_size("gz") - 1, 0.0, 1.0).astype(jnp.float32)
    inside = jnp.ones((padded.shape[4] - 2,), jnp.float32)
    scaling = jnp.concatenate([bottom[None], inside, topmost[None]])
    return padded * scaling


def apply_operator(jacobian, padded):
    extent_x = padded.shape[2] - 2
    extent_y = padded.shape[3] - 2
    extent_z = padded.shape[4] - 2
    total = jnp.zeros((padded.shape[0], padded.shape[1], extent_x, extent_y, extent_z), jnp.float32)
    for stencil_pos in range(27):
        start_x = stencil_pos // 9
        start_y = stencil_pos // 3 % 3
        start_z = stencil_pos % 3
        piece = padded[
            :,
            :,
            start_x : start_x + extent_x,
            start_y : start_y + extent_y,
            start_z : start_z + extent_z,
        ]
        block = jacobian[stencil_pos].astype(jnp.float32)
        for source_comp in range(block.shape[1]):
            total = total + block[None, :, source_comp] * piece[:, source_comp][:, None]
    return total


def shards(right_side, jacobian):
    field_shape = right_side.shape
    rhs_count = field_shape[0]
    flat_rhs = right_side.reshape(rhs_count, -1)
    start_matrix = one_axis_at_a_time(dot_high(flat_rhs, flat_rhs.T), GX_GY_GZ)
    start_factor = jnp.linalg.cholesky(start_matrix)
    basis = [lower_solve(start_factor, flat_rhs)]
    hessen_rows = []
    products = []
    for iteration in range(ITERS):
        workspace = apply_operator(jacobian, extend(basis[-1].reshape(field_shape))).reshape(
            rhs_count, -1
        )
        products.append(workspace)
        stacked = jnp.concatenate(basis, axis=0)
        coefficients, raw_gram = (
            one_axis_at_a_time(dot_high(stacked, workspace.T), GX_GY_GZ),
            one_axis_at_a_time(dot_high(workspace, workspace.T), GX_GY_GZ),
        )
        workspace = workspace - dot_high(coefficients.T, stacked)
        gram_matrix = raw_gram - dot_high(coefficients.T, coefficients)
        factor = jnp.linalg.cholesky(gram_matrix)
        basis.append(lower_solve(factor, workspace))
        filler = jnp.zeros((rhs_count, rhs_count * (ITERS - iteration - 1)), jnp.float32)
        hessen_rows.append(jnp.concatenate([coefficients.T, factor, filler], axis=1))
    hessen = jnp.concatenate(hessen_rows, axis=0)
    target = jnp.concatenate(
        [start_factor, jnp.zeros((rhs_count, rhs_count * ITERS), jnp.float32)], axis=1
    )
    normal_factor = jnp.linalg.cholesky(dot_high(hessen, hessen.T))
    middle = lower_solve(normal_factor, dot_high(hessen, target.T))
    weights = upper_solve(normal_factor, middle)
    solution = dot_high(weights.T, jnp.concatenate(basis[:-1], axis=0))
    solution_field = solution.reshape(field_shape)
    residual = right_side - apply_operator(jacobian, extend(solution_field))
    return (solution_field, residual)


def solution(mesh):
    split = Mesh(
        mesh.devices.reshape(4, 2, 2, mesh.shape["gy"], mesh.shape["gz"]),
        ("gx_0", "gx_1", "gx_2", "gy", "gz"),
    )
    in_specs = (P(None, None, GX, "gy", "gz"), P(None, None, None, GX, "gy", "gz"))
    out_specs = (P(None, None, GX, "gy", "gz"), P(None, None, GX, "gy", "gz"))
    return jax.shard_map(
        shards, mesh=split, in_specs=in_specs, out_specs=out_specs, check_vma=False
    )
```

profile of v0, /device:TPU:33, one launch (start us, length us, event | category | flops | bytes accessed | tf_op | source)
XLA Modules:
  0.0 498.9 jit_solution(1638787524583438542)
XLA Ops:
  2.1 8.5 %psum.245 = f32[4,4]{0,1:T(4,128)S(1)} all-reduce(f32[4,4]{0,1:T(4,128)S(1)} %convolution_bitcast_fusion.4), channel_id=1, replica_groups=mesh['gx_0'=4,'gx_1'=2,'gx_2'=2,'gy'=4,'gz'=4] {'gx_0'}, use_global_device_ids=true, to_apply=%region_0.0 | all-reduce | flops 16 | bytes 128 | tf_op jit(solution)/shard_map/psum | solution.py:31
  14.4 6.0 %psum.247 = f32[4,4]{0,1:T(4,128)S(1)} all-reduce(f32[4,4]{0,1:T(4,128)S(1)} %psum.246), channel_id=1, replica_groups=mesh['gx_0'=4,'gx_1'=2,'gx_2'=2,'gy'=4,'gz'=4] {'gx_2'}, use_global_device_ids=true, to_apply=%region_2.0 | all-reduce | flops 16 | bytes 128 | tf_op jit(solution)/shard_map/psum | solution.py:31
  20.3 8.7 %psum.248 = f32[4,4]{0,1:T(4,128)S(1)} all-reduce(f32[4,4]{0,1:T(4,128)S(1)} %psum.247), channel_id=1, replica_groups=mesh['gx_0'=4,'gx_1'=2,'gx_2'=2,'gy'=4,'gz'=4] {'gy'}, use_global_device_ids=true, to_apply=%region_3.0 | all-reduce | flops 16 | bytes 128 | tf_op jit(solution)/shard_map/psum | solution.py:31
  29.0 12.0 %psum.249 = f32[4,4]{0,1:T(4,128)S(1)} all-reduce(f32[4,4]{0,1:T(4,128)S(1)} %psum.248), channel_id=1, replica_groups=mesh['gx_0'=4,'gx_1'=2,'gx_2'=2,'gy'=4,'gz'=4] {'gz'}, use_global_device_ids=true, to_apply=%region_4.0 | all-reduce | flops 16 | bytes 128 | tf_op jit(solution)/shard_map/psum | solution.py:31
  48.0 5.4 %subtract_divide_fusion = (f32[1,5,1,8,128]{4,3,2,1,0:T(8,128)S(1)}, f32[1,5,1,8,128]{4,3,2,1,0:T(8,128)S(1)}, f32[1,5,1,8,128]{4,3,2,1,0:T(8,128)S(1)}, f32[1,5,1,8,128]{4,3,2,1,0:T(8,128)S(1)}) fusion(f32[1,5,1,8,128]{4,3,2,1,0:T(8,128)S(1)} %get-tuple-element.63, f32[1,5,1,8,128]{4,3,2,1,0:T(8,128)S(1)} %get-tuple-element.64, f32[]{:T(128)} %bitcast.16, ...), kind=kLoop, calls=%fused_computation.244 | loop fusion | flops 61440 | bytes 184348 | tf_op jit(solution)/shard_map/div | solution.py:44
  59.3 5.9 %subtract_divide_fusion.3 = (f32[1,5120]{1,0:T(1,128)S(1)}, f32[1,5120]{1,0:T(1,128)S(1)}, f32[1,5120]{1,0:T(1,128)S(1)}) fusion(f32[1,5120]{1,0:T(1,128)S(1)} %bitcast.1697, f32[1,5120]{1,0:T(1,128)S(1)} %bitcast.1646, f32[]{:T(128)} %bitcast.16, f32[]{:T(128)} %bitcast.15, f32[]{:T(128)} %bitcast.14, f32[]{:T(128)} %bitcast.13, f32[]{:T(128)} %bitcast.11, ...), kind=kLoop, calls=%fused_computation.248 | loop fusion | flops 76800 | bytes 143396 | tf_op jit(solution)/shard_map/div | solution.py:44
  72.3 9.8 %collective-permute-done.5 = f32[4,5,3,10,1]{4,3,2,1,0:T(8,128)S(1)} collective-permute-done((f32[4,5,3,10,1]{4,3,2,1,0:T(8,128)S(1)}, f32[4,5,3,10,1]{4,3,2,1,0:T(8,128)S(1)}, u32[]{:S(2)}, u32[]{:S(2)}) %collective-permute-start.5) | collective-permute-done | bytes 2432 | tf_op jit(solution)/shard_map/ppermute | solution.py:23
  82.0 5.4 %collective-permute-done.4 = f32[4,5,3,10,1]{4,3,2,1,0:T(8,128)S(1)} collective-permute-done((f32[4,5,3,10,1]{4,3,2,1,0:T(8,128)S(1)}, f32[4,5,3,10,1]{4,3,2,1,0:T(8,128)S(1)}, u32[]{:S(2)}, u32[]{:S(2)}) %collective-permute-start.4) | collective-permute-done | bytes 2432 | tf_op jit(solution)/shard_map/ppermute | solution.py:21
  92.1 16.1 %all-reduce.9 = (f32[4,4]{1,0:T(4,128)S(1)}, f32[4,4]{0,1:T(4,128)S(1)}) all-reduce(f32[4,4]{1,0:T(4,128)S(1)} %fusion.5, f32[4,4]{0,1:T(4,128)S(1)} %convolution_bitcast_fusion.3), channel_id=1, replica_groups=mesh['gx_0'=4,'gx_1'=2,'gx_2'=2,'gy'=4,'gz'=4] {'gx_0'}, use_global_device_ids=true, to_apply=%region_7.9 | all-reduce | flops 32 | bytes 256 | tf_op jit(solution)/shard_map/psum | solution.py:31
  111.9 5.7 %all-reduce.12 = (f32[4,4]{1,0:T(4,128)S(1)}, f32[4,4]{0,1:T(4,128)S(1)}) all-reduce(f32[4,4]{1,0:T(4,128)S(1)} %get-tuple-element.33, f32[4,4]{0,1:T(4,128)S(1)} %get-tuple-element.34), channel_id=1, replica_groups=mesh['gx_0'=4,'gx_1'=2,'gx_2'=2,'gy'=4,'gz'=4] {'gx_2'}, use_global_device_ids=true, to_apply=%region_9.11 | all-reduce | flops 32 | bytes 256 | tf_op jit(solution)/shard_map/psum | solution.py:31
  117.6 6.1 %all-reduce.6 = (f32[4,4]{1,0:T(4,128)S(1)}, f32[4,4]{0,1:T(4,128)S(1)}) all-reduce(f32[4,4]{1,0:T(4,128)S(1)} %get-tuple-element.27, f32[4,4]{0,1:T(4,128)S(1)} %get-tuple-element.28), channel_id=1, replica_groups=mesh['gx_0'=4,'gx_1'=2,'gx_2'=2,'gy'=4,'gz'=4] {'gy'}, use_global_device_ids=true, to_apply=%region_10.12 | all-reduce | flops 32 | bytes 256 | tf_op jit(solution)/shard_map/psum | solution.py:31
  123.7 7.1 %all-reduce.3 = (f32[4,4]{1,0:T(4,128)S(1)}, f32[4,4]{0,1:T(4,128)S(1)}) all-reduce(f32[4,4]{1,0:T(4,128)S(1)} %get-tuple-element.15, f32[4,4]{0,1:T(4,128)S(1)} %get-tuple-element.16), channel_id=1, replica_groups=mesh['gx_0'=4,'gx_1'=2,'gx_2'=2,'gy'=4,'gz'=4] {'gz'}, use_global_device_ids=true, to_apply=%region_11.13 | all-reduce | flops 32 | bytes 256 | tf_op jit(solution)/shard_map/psum | solution.py:31
  133.9 6.4 %fusion.23 = (f32[1,5120]{1,0:T(1,128)S(1)}, f32[1,5120]{1,0:T(1,128)S(1)}, f32[1,5120]{1,0:T(1,128)S(1)}, f32[1,5120]{1,0:T(1,128)S(1)}) fusion(f32[4,5120]{1,0:T(4,128)S(1)} %convolution_subtract_fusion.1, f32[]{:T(128)} %bitcast.355, f32[]{:T(128)} %bitcast.354, f32[]{:T(128)} %bitcast.353, f32[]{:T(128)} %bitcast.352, f32[]{:T(128)} %bitcast.351, ...), kind=kLoop, calls=%fused_computation.254 | loop fusion | flops 81920 | bytes 163880 | tf_op jit(solution)/shard_map/div | solution.py:44
  140.3 4.7 collective-permute-start.7
  159.4 21.2 %collective-permute-done.11 = f32[4,5,3,10,1]{4,3,2,1,0:T(8,128)} collective-permute-done((f32[4,5,3,10,1]{4,3,2,1,0:T(8,128)}, f32[4,5,3,10,1]{4,3,2,1,0:T(8,128)}, u32[]{:S(2)}, u32[]{:S(2)}) %collective-permute-start.11) | collective-permute-done | bytes 2432 | tf_op jit(solution)/shard_map/ppermute | solution.py:23
  189.0 6.8 %all-reduce.8 = (f32[8,4]{0,1:T(4,128)S(1)}, f32[4,4]{0,1:T(4,128)S(1)}) all-reduce(f32[8,4]{0,1:T(4,128)S(1)} %fusion.3, f32[4,4]{0,1:T(4,128)S(1)} %convolution_bitcast_fusion.2), channel_id=1, replica_groups=mesh['gx_0'=4,'gx_1'=2,'gx_2'=2,'gy'=4,'gz'=4] {'gx_0'}, use_global_device_ids=true, to_apply=%region_17.19 | all-reduce | flops 48 | bytes 384 | tf_op jit(solution)/shard_map/psum | solution.py:31
  199.6 5.8 %all-reduce.11 = (f32[8,4]{0,1:T(4,128)S(1)}, f32[4,4]{0,1:T(4,128)S(1)}) all-reduce(f32[8,4]{0,1:T(4,128)S(1)} %get-tuple-element.31, f32[4,4]{0,1:T(4,128)S(1)} %get-tuple-element.32), channel_id=1, replica_groups=mesh['gx_0'=4,'gx_1'=2,'gx_2'=2,'gy'=4,'gz'=4] {'gx_2'}, use_global_device_ids=true, to_apply=%region_19.21 | all-reduce | flops 48 | bytes 384 | tf_op jit(solution)/shard_map/psum | solution.py:31
  205.3 6.1 %all-reduce.5 = (f32[8,4]{0,1:T(4,128)S(1)}, f32[4,4]{0,1:T(4,128)S(1)}) all-reduce(f32[8,4]{0,1:T(4,128)S(1)} %get-tuple-element.25, f32[4,4]{0,1:T(4,128)S(1)} %get-tuple-element.26), channel_id=1, replica_groups=mesh['gx_0'=4,'gx_1'=2,'gx_2'=2,'gy'=4,'gz'=4] {'gy'}, use_global_device_ids=true, to_apply=%region_20.22 | all-reduce | flops 48 | bytes 384 | tf_op jit(solution)/shard_map/psum | solution.py:31
  211.4 7.2 %all-reduce.2 = (f32[8,4]{0,1:T(4,128)S(1)}, f32[4,4]{0,1:T(4,128)S(1)}) all-reduce(f32[8,4]{0,1:T(4,128)S(1)} %get-tuple-element.13, f32[4,4]{0,1:T(4,128)S(1)} %get-tuple-element.14), channel_id=1, replica_groups=mesh['gx_0'=4,'gx_1'=2,'gx_2'=2,'gy'=4,'gz'=4] {'gz'}, use_global_device_ids=true, to_apply=%region_21.23 | all-reduce | flops 48 | bytes 384 | tf_op jit(solution)/shard_map/psum | solution.py:31
  221.5 6.4 %fusion.24 = (f32[1,5120]{1,0:T(1,128)S(1)}, f32[1,5120]{1,0:T(1,128)S(1)}, f32[1,5120]{1,0:T(1,128)S(1)}, f32[1,5120]{1,0:T(1,128)S(1)}) fusion(f32[4,5120]{1,0:T(4,128)S(1)} %convolution_subtract_fusion, f32[]{:T(128)} %bitcast.511, f32[]{:T(128)} %bitcast.510, f32[]{:T(128)} %bitcast.509, f32[]{:T(128)} %bitcast.508, f32[]{:T(128)} %bitcast.507, ...), kind=kLoop, calls=%fused_computation.255 | loop fusion | flops 81920 | bytes 163880 | tf_op jit(solution)/shard_map/div | solution.py:44
  236.6 9.0 %collective-permute-start.14 = (f32[4,5,3,1,128]{4,3,2,1,0:T(1,128)S(1)}, f32[4,5,3,1,128]{4,3,2,1,0:T(1,128)S(1)}, u32[]{:S(2)}, u32[]{:S(2)}) collective-permute-start(f32[4,5,3,1,128]{4,3,2,1,0:T(1,128)S(1)} %get-tuple-element.645), channel_id=1, source_target_pairs={{0,4},{4,8},{8,12},{12,0},{1,5},{5,9},{9,13},{13,1},{2,6},{6,10},{... | collective-permute-start | bytes 92168 | tf_op jit(solution)/shard_map/ppermute | solution.py:21
  255.8 19.9 %collective-permute-done.17 = f32[4,5,3,10,1]{4,3,2,1,0:T(8,128)} collective-permute-done((f32[4,5,3,10,1]{4,3,2,1,0:T(8,128)}, f32[4,5,3,10,1]{4,3,2,1,0:T(8,128)}, u32[]{:S(2)}, u32[]{:S(2)}) %collective-permute-start.17) | collective-permute-done | bytes 2432 | tf_op jit(solution)/shard_map/ppermute | solution.py:23
  284.1 7.4 %all-reduce.7 = (f32[4,4]{0,1:T(4,128)S(1)}, f32[12,4]{0,1:T(4,128)S(1)}) all-reduce(f32[4,4]{0,1:T(4,128)S(1)} %convolution_bitcast_fusion.1, f32[12,4]{0,1:T(4,128)S(1)} %fusion), channel_id=1, replica_groups=mesh['gx_0'=4,'gx_1'=2,'gx_2'=2,'gy'=4,'gz'=4] {'gx_0'}, use_global_device_ids=true, to_apply=%region_32.34 | all-reduce | flops 64 | bytes 512 | tf_op jit(solution)/shard_map/psum | solution.py:31
  295.3 6.5 %all-reduce.10 = (f32[4,4]{0,1:T(4,128)S(1)}, f32[12,4]{0,1:T(4,128)S(1)}) all-reduce(f32[4,4]{0,1:T(4,128)S(1)} %get-tuple-element.29, f32[12,4]{0,1:T(4,128)S(1)} %get-tuple-element.30), channel_id=1, replica_groups=mesh['gx_0'=4,'gx_1'=2,'gx_2'=2,'gy'=4,'gz'=4] {'gx_2'}, use_global_device_ids=true, to_apply=%region_34.36 | all-reduce | flops 64 | bytes 512 | tf_op jit(solution)/shard_map/psum | solution.py:31
  301.8 6.1 %all-reduce.4 = (f32[4,4]{0,1:T(4,128)S(1)}, f32[12,4]{0,1:T(4,128)S(1)}) all-reduce(f32[4,4]{0,1:T(4,128)S(1)} %get-tuple-element.23, f32[12,4]{0,1:T(4,128)S(1)} %get-tuple-element.24), channel_id=1, replica_groups=mesh['gx_0'=4,'gx_1'=2,'gx_2'=2,'gy'=4,'gz'=4] {'gy'}, use_global_device_ids=true, to_apply=%region_35.37 | all-reduce | flops 64 | bytes 512 | tf_op jit(solution)/shard_map/psum | solution.py:31
  307.8 6.9 %all-reduce.1 = (f32[4,4]{0,1:T(4,128)S(1)}, f32[12,4]{0,1:T(4,128)S(1)}) all-reduce(f32[4,4]{0,1:T(4,128)S(1)} %get-tuple-element.11, f32[12,4]{0,1:T(4,128)S(1)} %get-tuple-element.12), channel_id=1, replica_groups=mesh['gx_0'=4,'gx_1'=2,'gx_2'=2,'gy'=4,'gz'=4] {'gz'}, use_global_device_ids=true, to_apply=%region_36.38 | all-reduce | flops 64 | bytes 512 | tf_op jit(solution)/shard_map/psum | solution.py:31
  324.5 41.0 %subtract_divide_fusion.18 = (f32[1,4]{0,1:T(4,128)S(1)}, f32[1,4]{0,1:T(4,128)S(1)}, f32[1,4]{0,1:T(4,128)S(1)}, f32[1,4]{0,1:T(4,128)S(1)}, f32[1,4]{0,1:T(4,1...) fusion(f32[12,4]{0,1:T(4,128)S(1)} %fusion.30, ...), kind=kLoop, calls=%fused_computation.833 | loop fusion | flops 484 | bytes 600 | tf_op jit(solution)/shard_map/div | solution.py:44
  365.5 30.2 %subtract_divide_fusion.9 = (f32[1,4]{0,1:T(4,128)S(1)}, f32[1,4]{0,1:T(4,128)S(1)}, f32[1,4]{0,1:T(4,128)S(1)}, f32[1,4]{0,1:T(4,128)S(1)}, f32[1,4]{0,1:T(4,12...) fusion(f32[1,4]{0,1:T(4,128)S(1)} %get-tuple-element.51, ...), kind=kLoop, calls=%fused_computation.824 | loop fusion | flops 416 | bytes 532 | tf_op jit(solution)/shard_map/div | solution.py:55
  395.7 26.1 %subtract_divide_fusion.6 = f32[1,4]{0,1:T(4,128)S(1)} fusion(f32[1,4]{0,1:T(4,128)S(1)} %get-tuple-element.43, f32[1,4]{0,1:T(4,128)S(1)} %get-tuple-element.42, f32[1,4]{0,1:T(4,128)S(1)} %get-tuple-element.41, f32[1,4]{0,1:T(4,128)S(1)} %get-tuple-element.40, f32[1,4]{0,1:T(4,128)S(1)} %get-tuple-element.39, f32[1,4]{0,1:T(4,128)S(1)} %get-tuple-element.38, ...), kind=kLoop, calls=%fused_computation.821 | loop fusion | flops 324 | bytes 376 | tf_op jit(solution)/shard_map/div | solution.py:55
  421.7 18.6 %subtract_divide_fusion.7 = f32[1,4]{0,1:T(4,128)S(1)} fusion(f32[1,4]{0,1:T(4,128)S(1)} %get-tuple-element.43, f32[1,4]{0,1:T(4,128)S(1)} %get-tuple-element.42, f32[1,4]{0,1:T(4,128)S(1)} %get-tuple-element.41, f32[1,4]{0,1:T(4,128)S(1)} %get-tuple-element.40, f32[1,4]{0,1:T(4,128)S(1)} %get-tuple-element.39, f32[1,4]{0,1:T(4,128)S(1)} %get-tuple-element.38, ...), kind=kLoop, calls=%fused_computation.822 | loop fusion | flops 228 | bytes 312 | tf_op jit(solution)/shard_map/div | solution.py:55
  440.3 11.9 %subtract_divide_fusion.8 = f32[1,4]{0,1:T(4,128)S(1)} fusion(f32[1,4]{0,1:T(4,128)S(1)} %get-tuple-element.43, f32[1,4]{0,1:T(4,128)S(1)} %get-tuple-element.42, f32[1,4]{0,1:T(4,128)S(1)} %get-tuple-element.41, f32[1,4]{0,1:T(4,128)S(1)} %get-tuple-element.40, f32[1,4]{0,1:T(4,128)S(1)} %get-tuple-element.39, f32[1,4]{0,1:T(4,128)S(1)} %get-tuple-element.38, ...), kind=kLoop, calls=%fused_computation.823 | loop fusion | flops 144 | bytes 252 | tf_op jit(solution)/shard_map/div | solution.py:55
  469.6 20.7 %collective-permute-done.23 = f32[4,5,3,10,1]{4,3,2,1,0:T(8,128)S(1)} collective-permute-done((f32[4,5,3,10,1]{4,3,2,1,0:T(8,128)S(1)}, f32[4,5,3,10,1]{4,3,2,1,0:T(8,128)S(1)}, u32[]{:S(2)}, u32[]{:S(2)}) %collective-permute-start.23) | collective-permute-done | bytes 2432 | tf_op jit(solution)/shard_map/ppermute | solution.py:23
  (194 shorter events, 130.9 us)
Async XLA Ops:
  0.6 58.3 %copy-start = (bf16[27,5,5,1,8,128]{5,4,3,2,1,0:T(8,128)(2,1)S(1)}, bf16[27,5,5,1,8,128]{5,4,3,2,1,0:T(8,128)(2,1)}, u32[]{:S(2)}) copy-start(bf16[27,5,5,1,8,128]{5,4,3,2,1,0:T(8,128)(2,1)} %param.4) | copy-start | bytes 4147204
  53.4 11.9 %collective-permute-start.1 = (f32[4,5,1,8,128]{4,3,2,1,0:T(8,128)S(1)}, f32[4,5,1,8,128]{4,3,2,1,0:T(8,128)S(1)}, u32[]{:S(2)}, u32[]{:S(2)}) collective-permute-start(f32[4,5,1,8,128]{4,3,2,1,0:T(8,128)S(1)} %pad_maximum_fusion.5), channel_id=1, source_target_pairs={{16,0},{32,16},{48,32},{64,48},{80,64},{96,80},{112,96},{128,112},... | collective-permute-start | bytes 245768 | tf_op jit(solution)/shard_map/ppermute | solution.py:23
  57.8 7.4 %collective-permute-start = (f32[4,5,1,8,128]{4,3,2,1,0:T(8,128)S(1)}, f32[4,5,1,8,128]{4,3,2,1,0:T(8,128)S(1)}, u32[]{:S(2)}, u32[]{:S(2)}) collective-permute-start(f32[4,5,1,8,128]{4,3,2,1,0:T(8,128)S(1)} %pad_maximum_fusion.5), channel_id=1, source_target_pairs={{0,16},{16,32},{32,48},{48,64},{64,80},{80,96},{96,112},{112,128},... | collective-permute-start | bytes 245768 | tf_op jit(solution)/shard_map/ppermute | solution.py:21
  65.3 2.8 collective-permute-start.3
  65.4 4.0 collective-permute-start.2
  69.7 12.3 %collective-permute-start.5 = (f32[4,5,3,10,1]{4,3,2,1,0:T(8,128)S(1)}, f32[4,5,3,10,1]{4,3,2,1,0:T(8,128)S(1)}, u32[]{:S(2)}, u32[]{:S(2)}) collective-permute-start(f32[4,5,3,10,1]{4,3,2,1,0:T(8,128)S(1)} %get-tuple-element.642), channel_id=1, source_target_pairs={{1,0},{2,1},{3,2},{0,3},{5,4},{6,5},{7,6},{4,7},{9,8},{10,9},{11,1... | collective-permute-start | bytes 7208 | tf_op jit(solution)/shard_map/ppermute | solution.py:23
  71.0 16.5 %collective-permute-start.4 = (f32[4,5,3,10,1]{4,3,2,1,0:T(8,128)S(1)}, f32[4,5,3,10,1]{4,3,2,1,0:T(8,128)S(1)}, u32[]{:S(2)}, u32[]{:S(2)}) collective-permute-start(f32[4,5,3,10,1]{4,3,2,1,0:T(8,128)S(1)} %get-tuple-element.641), channel_id=1, source_target_pairs={{0,1},{1,2},{2,3},{3,0},{4,5},{5,6},{6,7},{7,4},{8,9},{9,10},{10,1... | collective-permute-start | bytes 7208 | tf_op jit(solution)/shard_map/ppermute | solution.py:21
  130.8 9.5 %copy-start.4 = (f32[4,4]{1,0:T(4,128)}, f32[4,4]{1,0:T(4,128)S(1)}, u32[]{:S(2)}) copy-start(f32[4,4]{1,0:T(4,128)S(1)} %get-tuple-element.9) | copy-start | bytes 196
  140.3 9.4 %collective-permute-start.7 = (f32[4,5,1,8,128]{4,3,2,1,0:T(8,128)S(1)}, f32[4,5,1,8,128]{4,3,2,1,0:T(8,128)S(1)}, u32[]{:S(2)}, u32[]{:S(2)}) collective-permute-start(f32[4,5,1,8,128]{4,3,2,1,0:T(8,128)S(1)} %pad_maximum_fusion.6), channel_id=1, source_target_pairs={{16,0},{32,16},{48,32},{64,48},{80,64},{96,80},{112,96},{128,112},... | collective-permute-start | bytes 245768 | tf_op jit(solution)/shard_map/ppermute | solution.py:23
  145.0 4.7 collective-permute-start.6
  149.8 3.2 collective-permute-start.9
  151.2 4.4 collective-permute-start.8
  156.8 23.8 %collective-permute-start.11 = (f32[4,5,3,10,1]{4,3,2,1,0:T(8,128)}, f32[4,5,3,10,1]{4,3,2,1,0:T(8,128)}, u32[]{:S(2)}, u32[]{:S(2)}) collective-permute-start(f32[4,5,3,10,1]{4,3,2,1,0:T(8,128)} %get-tuple-element.640), channel_id=1, source_target_pairs={{1,0},{2,1},{3,2},{0,3},{5,4},{6,5},{7,6},{4,7},{9,8},{10,9},{11,1... | collective-permute-start | bytes 7208 | tf_op jit(solution)/shard_map/ppermute | solution.py:23
  158.2 24.9 %collective-permute-start.10 = (f32[4,5,3,10,1]{4,3,2,1,0:T(8,128)}, f32[4,5,3,10,1]{4,3,2,1,0:T(8,128)}, u32[]{:S(2)}, u32[]{:S(2)}) collective-permute-start(f32[4,5,3,10,1]{4,3,2,1,0:T(8,128)} %get-tuple-element.639), channel_id=1, source_target_pairs={{0,1},{1,2},{2,3},{3,0},{4,5},{5,6},{6,7},{7,4},{8,9},{9,10},{10,1... | collective-permute-start | bytes 7208 | tf_op jit(solution)/shard_map/ppermute | solution.py:21
  227.9 7.1 %collective-permute-start.13 = (f32[4,5,1,8,128]{4,3,2,1,0:T(8,128)S(1)}, f32[4,5,1,8,128]{4,3,2,1,0:T(8,128)S(1)}, u32[]{:S(2)}, u32[]{:S(2)}) collective-permute-start(f32[4,5,1,8,128]{4,3,2,1,0:T(8,128)S(1)} %pad_maximum_fusion.7), channel_id=1, source_target_pairs={{16,0},{32,16},{48,32},{64,48},{80,64},{96,80},{112,96},{128,112},... | collective-permute-start | bytes 245768 | tf_op jit(solution)/shard_map/ppermute | solution.py:23
  232.3 2.8 collective-permute-start.12
  235.1 10.5 %collective-permute-start.15 = (f32[4,5,3,1,128]{4,3,2,1,0:T(1,128)S(1)}, f32[4,5,3,1,128]{4,3,2,1,0:T(1,128)S(1)}, u32[]{:S(2)}, u32[]{:S(2)}) collective-permute-start(f32[4,5,3,1,128]{4,3,2,1,0:T(1,128)S(1)} %get-tuple-element.646), channel_id=1, source_target_pairs={{4,0},{8,4},{12,8},{0,12},{5,1},{9,5},{13,9},{1,13},{6,2},{10,6},{... | collective-permute-start | bytes 92168 | tf_op jit(solution)/shard_map/ppermute | solution.py:23
  236.6 18.1 %copy-start.5 = (f32[4,4]{1,0:T(4,128)S(1)}, f32[4,4]{1,0:T(4,128)}, u32[]{:S(2)}) copy-start(f32[4,4]{1,0:T(4,128)} %copy-done.4) | copy-start | bytes 196
  236.6 12.6 %collective-permute-start.14 = (f32[4,5,3,1,128]{4,3,2,1,0:T(1,128)S(1)}, f32[4,5,3,1,128]{4,3,2,1,0:T(1,128)S(1)}, u32[]{:S(2)}, u32[]{:S(2)}) collective-permute-start(f32[4,5,3,1,128]{4,3,2,1,0:T(1,128)S(1)} %get-tuple-element.645), channel_id=1, source_target_pairs={{0,4},{4,8},{8,12},{12,0},{1,5},{5,9},{9,13},{13,1},{2,6},{6,10},{... | collective-permute-start | bytes 92168 | tf_op jit(solution)/shard_map/ppermute | solution.py:21
  249.2 5.5 %copy-start.3 = (f32[4,5,3,1,128]{4,3,2,1,0:T(1,128)}, f32[4,5,3,1,128]{4,3,2,1,0:T(1,128)S(1)}, u32[]{:S(2)}) copy-start(f32[4,5,3,1,128]{4,3,2,1,0:T(1,128)S(1)} %collective-permute-done.14) | copy-start | bytes 92164
  250.4 25.3 %collective-permute-start.17 = (f32[4,5,3,10,1]{4,3,2,1,0:T(8,128)}, f32[4,5,3,10,1]{4,3,2,1,0:T(8,128)}, u32[]{:S(2)}, u32[]{:S(2)}) collective-permute-start(f32[4,5,3,10,1]{4,3,2,1,0:T(8,128)} %get-tuple-element.638), channel_id=1, source_target_pairs={{1,0},{2,1},{3,2},{0,3},{5,4},{6,5},{7,6},{4,7},{9,8},{10,9},{11,1... | collective-permute-start | bytes 7208 | tf_op jit(solution)/shard_map/ppermute | solution.py:23
  254.7 23.5 %collective-permute-start.16 = (f32[4,5,3,10,1]{4,3,2,1,0:T(8,128)}, f32[4,5,3,10,1]{4,3,2,1,0:T(8,128)}, u32[]{:S(2)}, u32[]{:S(2)}) collective-permute-start(f32[4,5,3,10,1]{4,3,2,1,0:T(8,128)} %get-tuple-element.637), channel_id=1, source_target_pairs={{0,1},{1,2},{2,3},{3,0},{4,5},{5,6},{6,7},{7,4},{8,9},{9,10},{10,1... | collective-permute-start | bytes 7208 | tf_op jit(solution)/shard_map/ppermute | solution.py:21
  281.1 35.6 %copy-start.6 = (f32[4,4]{1,0:T(4,128)S(1)}, f32[4,4]{1,0:T(4,128)}, u32[]{:S(2)}) copy-start(f32[4,4]{1,0:T(4,128)} %copy.13) | copy-start | bytes 196
  452.7 41.2 %copy-start.1 = (f32[1,4,40,128]{3,2,1,0:T(8,128)}, f32[1,4,40,128]{3,2,1,0:T(8,128)S(1)}, u32[]{:S(2)}) copy-start(f32[1,4,40,128]{3,2,1,0:T(8,128)S(1)} %copy.75) | copy-start | bytes 245764
  452.7 7.1 %collective-permute-start.19 = (f32[4,5,1,8,128]{4,3,2,1,0:T(8,128)S(1)}, f32[4,5,1,8,128]{4,3,2,1,0:T(8,128)S(1)}, u32[]{:S(2)}, u32[]{:S(2)}) collective-permute-start(f32[4,5,1,8,128]{4,3,2,1,0:T(8,128)S(1)} %bitcast.1651), channel_id=1, source_target_pairs={{16,0},{32,16},{48,32},{64,48},{80,64},{96,80},{112,96},{128,112},... | collective-permute-start | bytes 245768 | tf_op jit(solution)/shard_map/ppermute | solution.py:23
  456.8 3.1 collective-permute-start.18
  459.9 3.1 collective-permute-start.21
  461.7 4.1 collective-permute-start.20
  466.1 24.2 %collective-permute-start.23 = (f32[4,5,3,10,1]{4,3,2,1,0:T(8,128)S(1)}, f32[4,5,3,10,1]{4,3,2,1,0:T(8,128)S(1)}, u32[]{:S(2)}, u32[]{:S(2)}) collective-permute-start(f32[4,5,3,10,1]{4,3,2,1,0:T(8,128)S(1)} %get-tuple-element.636), channel_id=1, source_target_pairs={{1,0},{2,1},{3,2},{0,3},{5,4},{6,5},{7,6},{4,7},{9,8},{10,9},{11,1... | collective-permute-start | bytes 7208 | tf_op jit(solution)/shard_map/ppermute | solution.py:23
  469.6 24.3 %collective-permute-start.22 = (f32[4,5,3,10,1]{4,3,2,1,0:T(8,128)S(1)}, f32[4,5,3,10,1]{4,3,2,1,0:T(8,128)S(1)}, u32[]{:S(2)}, u32[]{:S(2)}) collective-permute-start(f32[4,5,3,10,1]{4,3,2,1,0:T(8,128)S(1)} %get-tuple-element.635), channel_id=1, source_target_pairs={{0,1},{1,2},{2,3},{3,0},{4,5},{5,6},{6,7},{7,4},{8,9},{9,10},{10,1... | collective-permute-start | bytes 7208 | tf_op jit(solution)/shard_map/ppermute | solution.py:21
  495.0 0.9 copy-start.2
where the time goes:
time: 506 us; the launch traced here: 499 us
  other arithmetic  182 us (36%)
  blocking collectives  138 us (27%)
  waiting for transfers between devices  107 us (21%)
  starting transfers between devices  49.7 us (10%)
  local copies, waits for them, and re-layouts  14.4 us (3%)
  matrix products  6.06 us (1%)
    psum x20, blocking collectives, one_axis_at_a_time(): return functools.reduce(lax.psum, axes, value)  138 us
    div x4, other arithmetic, upper_solve(): solved[row_pos] = accum / factor[row_pos, row_pos]  86.8 us
    ppermute x12, waiting for transfers between devices, extended(): lax.ppermute(head, axis, [((i + 1) % count, i) for i in range(count)])  82.2 us
    div x6, other arithmetic, lower_solve(): solved.append(accum / factor[row_pos, row_pos])  69.6 us
    ppermute x12, starting transfers between devices, extended(): lax.ppermute(head, axis, [((i + 1) % count, i) for i in range(count)])  32.9 us
    ppermute x12, waiting for transfers between devices, extended(): lax.ppermute(tail, axis, [(i, (i + 1) % count) for i in range(count)])  24.4 us
    ppermute x12, starting transfers between devices, extended(): lax.ppermute(tail, axis, [(i, (i + 1) % count) for i in range(count)])  16.8 us
  transfers between devices with their start and end apart: 24, of which 18 were waited for; matrix products, arithmetic and copies ran while one was open for 2% of the time, Pallas kernels for 0%

commit v1 on v0

v1 whole, which is shorter than its diff:
```python
import jax
import jax.numpy as jnp
from jax import lax
from jax.experimental import pallas as pl
from jax.experimental.pallas import tpu as pltpu
from jax.sharding import PartitionSpec as P

MESH = pl.DeviceIdType.MESH
SHIFT = 9.0
BETA1 = 3.9
BETA2 = 3.2
STEPS = 3
ROW = 8

OFFSETS = [
    (ex, ey, ez)
    for ey, ez in ((0, 0), (0, -1), (0, 1), (-1, 0), (1, 0), (-1, -1), (-1, 1), (1, -1), (1, 1))
    for ex in (-1, 1, 0)
    if (ex, ey, ez) != (0, 0, 0)
]


def side(sign):
    return (sign + 1) // 2


def make_kernel(nx, ny, nz):
    group_a = (nx // 4) * ny
    group_b = 4 * nz

    def kernel(
        rhs_ref, jac_hbm, sol_ref, res_ref,
        jac_raw, jac, basis, slab, rowbuf, colbuf, corbuf, rowsrc, colsrc, corsrc, padded,
        gramsrc, sumsrc, gather_a, gather_b,
        jac_sem, halo_send, halo_recv, a_send, a_recv, b_send, b_recv,
    ):
        ix, iy, iz = lax.axis_index("gx"), lax.axis_index("gy"), lax.axis_index("gz")

        def neighbour(offset):
            ex, ey, ez = offset
            return (
                lax.rem(ix + ex + nx, nx),
                lax.rem(iy + ey + ny, ny),
                lax.rem(iz + ez + nz, nz),
            )

        rank_a = (ix // 4) * ny + iy
        rank_b = lax.rem(ix, 4) * nz + iz

        def partner_a(offset):
            rank = lax.rem(rank_a + offset, group_a)
            return ((rank // ny) * 4 + lax.rem(ix, 4), lax.rem(rank, ny), iz)

        def partner_b(offset):
            rank = lax.rem(rank_b + offset, group_b)
            return ((ix // 4) * 4 + rank // nz, iy, lax.rem(rank, nz))

        jac_copy = pltpu.make_async_copy(jac_hbm, jac_raw, jac_sem)
        jac_copy.start()

        barrier = pltpu.get_barrier_semaphore()
        partners = [neighbour(offset) for offset in OFFSETS]
        partners += [partner_a(offset) for offset in range(1, group_a)]
        partners += [partner_b(offset) for offset in range(1, group_b)]
        for partner in partners:
            pl.semaphore_signal(barrier, inc=1, device_id=partner, device_id_type=MESH)

        lane = lax.broadcasted_iota(jnp.int32, (8, 128), 1)
        lane3 = lax.broadcasted_iota(jnp.int32, (4, 8, 128), 2)
        at_low = iz == 0
        at_high = iz == nz - 1

        def halo_copies(step):
            copies = []
            for index, offset in enumerate(OFFSETS):
                ex, ey, ez = offset
                if ey == 0 and ez == 0:
                    src, dst = basis.at[step], slab.at[step, side(-ex)]
                elif ez == 0:
                    src, dst = rowsrc.at[step, side(ey)], rowbuf.at[step, 1 - ex, side(-ey)]
                elif ey == 0:
                    src, dst = colsrc.at[step, side(ez)], colbuf.at[step, 1 - ex, side(-ez)]
                else:
                    src = corsrc.at[step, 2 * side(ey) + side(ez)]
                    dst = corbuf.at[step, 1 - ex, 2 * side(-ey) + side(-ez)]
                copies.append(
                    pltpu.make_async_remote_copy(
                        src_ref=src,
                        dst_ref=dst,
                        send_sem=halo_send.at[step, index],
                        recv_sem=halo_recv.at[step, index],
                        device_id=neighbour(offset),
                        device_id_type=MESH,
                    )
                )
            return copies

        def pack(step):
            low = jnp.zeros((8, 128), jnp.float32)
            high = jnp.zeros((8, 128), jnp.float32)
            for r in range(4):
                for b in range(5):
                    field = 5 * r + b
                    tile = basis[step, r, b]
                    low = jnp.where(lane == field, pltpu.roll(tile, field, 1) if field else tile, low)
                    high = jnp.where(lane == field, pltpu.roll(tile, field + 1, 1), high)
                    rowsrc[step, 0, field : field + 1, :] = tile[0:1, :]
                    rowsrc[step, 1, field : field + 1, :] = tile[7:8, :]
            colsrc[step, 0] = low
            colsrc[step, 1] = high
            for pos in range(2):
                edge = slice(7 * pos, 7 * pos + 1)
                corsrc[step, 2 * pos] = low[edge, :]
                corsrc[step, 2 * pos + 1] = high[edge, :]

        row_id = lax.broadcasted_iota(jnp.int32, (24, 128), 0)
        lane_row = lax.broadcasted_iota(jnp.int32, (24, 128), 1)

        def fill(step, plane, source):
            for dz in (-1, 0, 1):
                if dz != 0:
                    column = colbuf[step, plane, side(dz)]
                    outside = at_low if dz < 0 else at_high
                    column = jnp.where(outside, jnp.zeros_like(column), column)
                    edge_lane = 0 if dz < 0 else 127
                    turn = 1 if dz < 0 else 127
                for r in range(4):
                    for b in range(5):
                        tile = source[r, b]
                        if dz != 0:
                            field = 5 * r + b
                            shift = (edge_lane - field) % 128
                            moved = pltpu.roll(column, shift, 1) if shift else column
                            tile = jnp.where(lane == edge_lane, moved, pltpu.roll(tile, turn, 1))
                        padded[plane, dz + 1, r, b, ROW : ROW + 8, :] = tile
                for dy in (-1, 1):
                    rows = rowbuf[step, plane, side(dy)]
                    if dz != 0:
                        corner = corbuf[step, plane, 2 * side(dy) + side(dz)]
                        spread = jnp.broadcast_to(corner, (24, 128))
                        spread = jnp.where(row_id == lane_row, spread, 0.0)
                        corner_column = jnp.sum(spread, axis=1, keepdims=True)
                        corner_column = jnp.where(outside, jnp.zeros_like(corner_column), corner_column)
                        rows = jnp.where(lane_row == edge_lane, corner_column, pltpu.roll(rows, turn, 1))
                    target = ROW - 1 if dy < 0 else ROW + 8
                    for r in range(4):
                        for b in range(5):
                            field = 5 * r + b
                            padded[plane, dz + 1, r, b, target : target + 1, :] = rows[field : field + 1, :]

        def accumulate(plane, totals):
            def at_dz(dzi, totals):
                totals = list(totals)
                for dyi in range(3):
                    start = ROW - 1 + dyi
                    s = plane * 9 + dyi * 3 + dzi
                    for b in range(5):
                        values = padded[plane, dzi, :, b, start : start + 8, :]
                        for a in range(5):
                            totals[a] = totals[a] + jac[s * 25 + 5 * a + b][None] * values
                return tuple(totals)

            return lax.fori_loop(0, 3, at_dz, totals)

        def gram_block(block):
            gram = jnp.zeros((4, 128), jnp.float32)
            lanes = lax.broadcasted_iota(jnp.int32, (4, 128), 1)
            for n in range(4 * block + 4):
                product = basis[block, :, 0] * basis[n // 4, n % 4, 0][None]
                for b in range(1, 5):
                    product = product + basis[block, :, b] * basis[n // 4, n % 4, b][None]
                partial = jnp.sum(jnp.sum(product, axis=1), axis=1, keepdims=True)
                gram = jnp.where(lanes == 16 * block + n, partial, gram)
            return gram

        basis[0] = rhs_ref[...]
        pack(0)
        jac_copy.wait()

        def unpack(s, carry):
            rows = pl.ds(s * 25, 25)
            jac[rows] = jac_raw[rows].astype(jnp.float32)
            return carry

        lax.fori_loop(0, 27, unpack, 0)
        for a in range(5):
            jac[13 * 25 + 6 * a] = jac[13 * 25 + 6 * a] - SHIFT

        pl.semaphore_wait(barrier, len(partners))

        sent = []
        gram = jnp.zeros((4, 128), jnp.float32)
        for step in range(STEPS):
            copies = halo_copies(step)
            for copy in copies:
                copy.start()
            sent += copies
            gram = gram + gram_block(step)
            totals = tuple(jnp.zeros((4, 8, 128), jnp.float32) for _ in range(5))
            for plane in (1, 0, 2):
                for copy, offset in zip(copies, OFFSETS):
                    if 1 - offset[0] == plane:
                        copy.wait_recv()
                fill(step, plane, basis.at[step] if plane == 1 else slab.at[step, plane // 2])
                totals = accumulate(plane, totals)
            for a in range(5):
                value = totals[a]
                if step == 1:
                    value = value - BETA1 * basis[0, :, a]
                if step == 2:
                    value = value - BETA2 * basis[1, :, a]
                basis[step + 1, :, a] = value
            if step + 1 < STEPS:
                pack(step + 1)
        gram = gram + gram_block(3)

        def gather(partial, size, rank, partner, src, slots, send, recv):
            src[...] = partial
            slots[rank] = partial
            copies = []
            for offset in range(1, size):
                copies.append(
                    pltpu.make_async_remote_copy(
                        src_ref=src,
                        dst_ref=slots.at[rank],
                        send_sem=send.at[offset],
                        recv_sem=recv.at[offset],
                        device_id=partner(offset),
                        device_id_type=MESH,
                    )
                )
            for copy in copies:
                copy.start()
            for copy in copies:
                copy.wait_recv()
            parts = [slots[i] for i in range(size)]
            while len(parts) > 1:
                parts = [parts[i] + parts[i + 1] if i + 1 < len(parts) else parts[i] for i in range(0, len(parts), 2)]
            return parts[0], copies

        gram, copies = gather(gram, group_a, rank_a, partner_a, gramsrc, gather_a, a_send, a_recv)
        sent += copies
        gram, copies = gather(gram, group_b, rank_b, partner_b, sumsrc, gather_b, b_send, b_recv)
        sent += copies

        size = 4 * (STEPS + 1)
        row = lax.broadcasted_iota(jnp.int32, (size, 128), 0)
        columns = []
        for n in range(size):
            pieces = []
            for block in range(STEPS + 1):
                if n < 4 * block + 4:
                    at = 16 * block + n
                    pieces.append(jnp.broadcast_to(gram[:, at : at + 1], (4, 128)))
                else:
                    pieces.append(jnp.zeros((4, 128), jnp.float32))
            columns.append(jnp.concatenate(pieces, axis=0))
        at_zero = [
            1.0,
            -SHIFT,
            SHIFT * SHIFT - BETA1,
            -SHIFT * SHIFT * SHIFT + SHIFT * (BETA1 + BETA2),
        ]
        rights = []
        for r in range(4):
            value = jnp.zeros((size, 128), jnp.float32)
            for block in range(STEPS + 1):
                value = jnp.where(row == 4 * block + r, at_zero[block], value)
            rights.append(value)
        inverses = []
        factors = []
        for k in range(size):
            column = columns[k]
            inverse = 1.0 / column[k : k + 1, :]
            factor = jnp.where(row > k, column * inverse, 0.0)
            inverses.append(inverse)
            factors.append(factor)
            for j in range(k + 1, size):
                columns[j] = columns[j] - factor * column[j : j + 1, :]
            for r in range(4):
                rights[r] = rights[r] - factor * rights[r][k : k + 1, :]
        for r in range(4):
            value = rights[r]
            scale = jnp.concatenate(inverses, axis=0)
            value = value * scale
            for k in range(size - 2, -1, -1):
                below = jnp.sum(factors[k] * value, axis=0, keepdims=True)
                value = value - jnp.where(row == k, below, 0.0)
            rights[r] = value
        small = []
        for r in range(4):
            value = at_zero[0] * rights[r][0:4]
            for block in range(1, STEPS + 1):
                value = value + at_zero[block] * rights[r][4 * block : 4 * block + 4]
            small.append(value)
        for k in range(4):
            inverse = 1.0 / small[k][k : k + 1, :]
            small[k] = small[k] * inverse
            rights[k] = rights[k] * inverse
            for r in range(4):
                if r != k:
                    scale = small[r][k : k + 1, :]
                    small[r] = small[r] - scale * small[k]
                    rights[r] = rights[r] - scale * rights[k]

        for r in range(4):
            c = [[rights[r][4 * block + q : 4 * block + q + 1, :] for q in range(4)] for block in range(4)]
            d = [[], [], []]
            for q in range(4):
                d[0].append(SHIFT * c[2][q] - c[1][q] - (SHIFT * SHIFT - BETA2) * c[3][q])
                d[1].append(SHIFT * c[3][q] - c[2][q])
                d[2].append(-c[3][q])
            residual = jnp.zeros((5, 8, 128), jnp.float32)
            answer = jnp.zeros((5, 8, 128), jnp.float32)
            for block in range(4):
                for q in range(4):
                    values = basis[block, q]
                    residual = residual + values * c[block][q][None]
                    if block < 3:
                        answer = answer + values * d[block][q][None]
            res_ref[r] = residual
            sol_ref[r] = answer

        for copy in sent:
            copy.wait_send()

    return kernel, group_a, group_b


def solution(mesh):
    nx, ny, nz = mesh.shape["gx"], mesh.shape["gy"], mesh.shape["gz"]
    kernel, group_a, group_b = make_kernel(nx, ny, nz)
    f32 = jnp.float32
    count = len(OFFSETS)

    def shards(right_side, jacobian):
        field = jax.ShapeDtypeStruct((4, 5, 8, 128), f32)
        answer, residual = pl.pallas_call(
            kernel,
            out_shape=(field, field),
            in_specs=[
                pl.BlockSpec(memory_space=pltpu.VMEM),
                pl.BlockSpec(memory_space=pl.ANY),
            ],
            out_specs=(
                pl.BlockSpec(memory_space=pltpu.VMEM),
                pl.BlockSpec(memory_space=pltpu.VMEM),
            ),
            scratch_shapes=[
                pltpu.VMEM((675, 8, 128), jnp.bfloat16),
                pltpu.VMEM((675, 8, 128), f32),
                pltpu.VMEM((STEPS + 1, 4, 5, 8, 128), f32),
                pltpu.VMEM((STEPS, 2, 4, 5, 8, 128), f32),
                pltpu.VMEM((STEPS, 3, 2, 24, 128), f32),
                pltpu.VMEM((STEPS, 3, 2, 8, 128), f32),
                pltpu.VMEM((STEPS, 3, 4, 1, 128), f32),
                pltpu.VMEM((STEPS, 2, 24, 128), f32),
                pltpu.VMEM((STEPS, 2, 8, 128), f32),
                pltpu.VMEM((STEPS, 4, 1, 128), f32),
                pltpu.VMEM((3, 3, 4, 5, 24, 128), f32),
                pltpu.VMEM((4, 128), f32),
                pltpu.VMEM((4, 128), f32),
                pltpu.VMEM((group_a, 4, 128), f32),
                pltpu.VMEM((group_b, 4, 128), f32),
                pltpu.SemaphoreType.DMA,
                pltpu.SemaphoreType.DMA((STEPS, count)),
                pltpu.SemaphoreType.DMA((STEPS, count)),
                pltpu.SemaphoreType.DMA((group_a,)),
                pltpu.SemaphoreType.DMA((group_a,)),
                pltpu.SemaphoreType.DMA((group_b,)),
                pltpu.SemaphoreType.DMA((group_b,)),
            ],
            compiler_params=pltpu.CompilerParams(
                collective_id=0, has_side_effects=True, vmem_limit_bytes=40 * 1024 * 1024
            ),
        )(right_side.reshape(4, 5, 8, 128), jacobian.reshape(675, 8, 128))
        return answer.reshape(right_side.shape), residual.reshape(right_side.shape)

    return jax.shard_map(
        shards,
        mesh=mesh,
        in_specs=(P(None, None, "gx", "gy", "gz"), P(None, None, None, "gx", "gy", "gz")),
        out_specs=(P(None, None, "gx", "gy", "gz"), P(None, None, "gx", "gy", "gz")),
        check_vma=False,
    )
```

time: 506 us -> 52.6 us (0.10)
  the two profiles are of different devices: /device:TPU:33 before, /device:TPU:1 now
where the time goes in v1:
time: 52.6 us; the launch traced here: 52.5 us
  Pallas kernels  48.3 us (92%)
  local copies, waits for them, and re-layouts  3.49 us (7%)
  between operations  0.65 us (1%)
    pallas_call x1, Pallas kernels, shards(): pl.pallas_call(kernel, out_shape=(field, field), in_specs=[pl.BlockSpec(m...  48.3 us
    unnamed x6, local copies, waits for them, and re-layouts  3.49 us

profile of v1, /device:TPU:1, one launch (start us, length us, event | category | flops | bytes accessed | tf_op | source)
XLA Modules:
  0.0 52.5 jit_solution(10327034194997813954)
XLA Ops:
  0.6 0.0 copy-start
  0.6 1.3 %copy-done = bf16[27,5,5,1,8,128]{5,4,3,2,1,0:T(8,128)(2,1)S(1)} copy-done((bf16[27,5,5,1,8,128]{5,4,3,2,1,0:T(8,128)(2,1)S(1)}, bf16[27,5,5,1,8,128]{5,4,3,2,1,0:T(8,128)(2,1)}, u32[]{:S(2)}) %copy-start) | copy-done | bytes 1382424
  2.0 0.0 copy-start.1
  2.0 0.9 %copy-done.1 = f32[4,5,1,8,128]{4,3,2,1,0:T(8,128)S(1)} copy-done((f32[4,5,1,8,128]{4,3,2,1,0:T(8,128)S(1)}, f32[4,5,1,8,128]{4,3,2,1,0:T(8,128)}, u32[]{:S(2)}) %copy-start.1) | copy-done | bytes 81944
  2.9 48.3 %shard_map.41 = (f32[4,5,8,128]{3,2,1,0:T(8,128)S(1)}, f32[4,5,8,128]{3,2,1,0:T(8,128)S(1)}) custom-call(f32[4,5,8,128]{3,2,1,0:T(8,128)S(1)} %bitcast.9, bf16[675,8,128]{2,1,0:T(8,128)(2,1)S(1)} %bitcast.8), custom_call_target="tpu_custom_call" | custom-call | tf_op jit(solution)/shard_map/pallas_call | solution.py:338
  51.2 0.6 %copy.8 = f32[4,5,1,8,128]{4,3,2,1,0:T(8,128)} copy(f32[4,5,1,8,128]{4,3,2,1,0:T(8,128)S(1)} %bitcast.11) | data formatting | bytes 163840
  51.8 0.6 %copy.9 = f32[4,5,1,8,128]{4,3,2,1,0:T(8,128)} copy(f32[4,5,1,8,128]{4,3,2,1,0:T(8,128)S(1)} %bitcast.10) | data formatting | bytes 163840
Async XLA Ops:
  0.6 1.3 %copy-start = (bf16[27,5,5,1,8,128]{5,4,3,2,1,0:T(8,128)(2,1)S(1)}, bf16[27,5,5,1,8,128]{5,4,3,2,1,0:T(8,128)(2,1)}, u32[]{:S(2)}) copy-start(bf16[27,5,5,1,8,128]{5,4,3,2,1,0:T(8,128)(2,1)} %param.3) | copy-start | bytes 4147204
  2.0 0.9 %copy-start.1 = (f32[4,5,1,8,128]{4,3,2,1,0:T(8,128)S(1)}, f32[4,5,1,8,128]{4,3,2,1,0:T(8,128)}, u32[]{:S(2)}) copy-start(f32[4,5,1,8,128]{4,3,2,1,0:T(8,128)} %param.2) | copy-start | bytes 245764

commit v2 on v1

--- a/solution.py
+++ b/solution.py
@@ -14,7 +14,7 @@
 
 OFFSETS = [
     (ex, ey, ez)
-    for ey, ez in ((0, 0), (0, -1), (0, 1), (-1, 0), (1, 0), (-1, -1), (-1, 1), (1, -1), (1, 1))
+    for ey, ez in ((-1, -1), (-1, 1), (1, -1), (1, 1), (0, -1), (0, 1), (-1, 0), (1, 0), (0, 0))
     for ex in (-1, 1, 0)
     if (ex, ey, ez) != (0, 0, 0)
 ]
@@ -29,10 +29,10 @@
     group_b = 4 * nz
 
     def kernel(
-        rhs_ref, jac_hbm, sol_ref, res_ref,
+        rhs_hbm, jac_hbm, sol_ref, res_ref,
         jac_raw, jac, basis, slab, rowbuf, colbuf, corbuf, rowsrc, colsrc, corsrc, padded,
         gramsrc, sumsrc, gather_a, gather_b,
-        jac_sem, halo_send, halo_recv, a_send, a_recv, b_send, b_recv,
+        rhs_sem, jac_sem, halo_send, halo_recv, a_send, a_recv, b_send, b_recv,
     ):
         ix, iy, iz = lax.axis_index("gx"), lax.axis_index("gy"), lax.axis_index("gz")
 
@@ -55,6 +55,8 @@
             rank = lax.rem(rank_b + offset, group_b)
             return ((ix // 4) * 4 + rank // nz, iy, lax.rem(rank, nz))
 
+        rhs_copy = pltpu.make_async_copy(rhs_hbm, basis.at[0], rhs_sem)
+        rhs_copy.start()
         jac_copy = pltpu.make_async_copy(jac_hbm, jac_raw, jac_sem)
         jac_copy.start()
 
@@ -173,7 +175,7 @@
                 gram = jnp.where(lanes == 16 * block + n, partial, gram)
             return gram
 
-        basis[0] = rhs_ref[...]
+        rhs_copy.wait()
         pack(0)
         jac_copy.wait()
 
@@ -339,8 +341,8 @@
             kernel,
             out_shape=(field, field),
             in_specs=[
-                pl.BlockSpec(memory_space=pltpu.VMEM),
-                pl.BlockSpec(memory_space=pl.ANY),
+                pl.BlockSpec(memory_space=pltpu.HBM),
+                pl.BlockSpec(memory_space=pltpu.HBM),
             ],
             out_specs=(
                 pl.BlockSpec(memory_space=pltpu.VMEM),
@@ -363,6 +365,7 @@
                 pltpu.VMEM((group_a, 4, 128), f32),
                 pltpu.VMEM((group_b, 4, 128), f32),
                 pltpu.SemaphoreType.DMA,
+                pltpu.SemaphoreType.DMA,
                 pltpu.SemaphoreType.DMA((STEPS, count)),
                 pltpu.SemaphoreType.DMA((STEPS, count)),
                 pltpu.SemaphoreType.DMA((group_a,)),
@@ -371,7 +374,7 @@
                 pltpu.SemaphoreType.DMA((group_b,)),
             ],
             compiler_params=pltpu.CompilerParams(
-                collective_id=0, has_side_effects=True, vmem_limit_bytes=40 * 1024 * 1024
+                collective_id=0, has_side_effects=True, vmem_limit_bytes=56360960
             ),
         )(right_side.reshape(4, 5, 8, 128), jacobian.reshape(675, 8, 128))
         return answer.reshape(right_side.shape), residual.reshape(right_side.shape)

time: 52.6 us -> 44.6 us (0.85)
  Pallas kernels: 48.3 us -> 42.5 us
  local copies, waits for them, and re-layouts: 3.49 us -> 1.27 us
    pallas_call x1, Pallas kernels: 48.3 us -> 42.5 us  [shards(): pl.pallas_call(kernel, out_shape=(field, field), in_specs=[pl.BlockSpec(m...]
    unnamed x6 -> x2, local copies, waits for them, and re-layouts: 3.49 us -> 1.27 us
where the time goes in v2:
time: 44.6 us; the launch traced here: 44.5 us
  Pallas kernels  42.5 us (95%)
  local copies, waits for them, and re-layouts  1.27 us (3%)
  between operations  0.64 us (1%)
    pallas_call x1, Pallas kernels, shards(): pl.pallas_call(kernel, out_shape=(field, field), in_specs=[pl.BlockSpec(m...  42.5 us
    unnamed x2, local copies, waits for them, and re-layouts  1.27 us

profile of v2, /device:TPU:1, one launch (start us, length us, event | category | flops | bytes accessed | tf_op | source)
XLA Modules:
  0.0 44.5 jit_solution(12572285100080397955)
XLA Ops:
  0.6 42.5 %shard_map.41 = (f32[4,5,8,128]{3,2,1,0:T(8,128)S(1)}, f32[4,5,8,128]{3,2,1,0:T(8,128)S(1)}) custom-call(f32[4,5,8,128]{3,2,1,0:T(8,128)} %bitcast.11, bf16[675,8,128]{2,1,0:T(8,128)(2,1)} %bitcast.10), custom_call_target="tpu_custom_call" | custom-call | tf_op jit(solution)/shard_map/pallas_call | solution.py:340
  43.2 0.6 %copy.8 = f32[4,5,1,8,128]{4,3,2,1,0:T(8,128)} copy(f32[4,5,1,8,128]{4,3,2,1,0:T(8,128)S(1)} %bitcast.9) | data formatting | bytes 163840
  43.8 0.6 %copy.9 = f32[4,5,1,8,128]{4,3,2,1,0:T(8,128)} copy(f32[4,5,1,8,128]{4,3,2,1,0:T(8,128)S(1)} %bitcast.8) | data formatting | bytes 163840
